TPU v7x, 512 devices: a 8x2x16 block of a 8x8x16 slice. The times are simulated.
512 devices in a mesh: groups: 2 (over y), rows: 16 (over z), cols: 8 (over x), sub: 2 (over core).
Axes of the slice: x: 8, y: 2, z: 16, core: 2. Of those that a mesh axis runs over, the one named last changes fastest.
The devices are a block of a 8x8x16 slice.
Arguments:
- stored_vectors: bfloat16 [3072, 131072], P(('cols', 'sub'), ('groups', 'rows')), parts along dimension 1, may hold values from -0.59765625 to 0.59765625
- previous_columns: bfloat16 [131072, 256], P(('groups', 'rows', 'cols', 'sub')), parts along dimension 0, may hold values from -3 to 3
- pivots: int32 [512], P('groups'), parts along dimension 0, may hold values from 0 to 65535, as said below
- diagonal: float32 [131072], P(('groups', 'rows', 'cols', 'sub')), parts along dimension 0, may hold values from 2 to 32
- ket_blocks: bfloat16 [2048, 128, 256], P(('groups', 'rows', 'cols', 'sub')), parts along dimension 0, may hold values from -6 to 6
- shell_tags: int32 [2048, 128], P(('groups', 'rows', 'cols', 'sub')), parts along dimension 0, may hold values from 0 to 3
- target_blocks: int32 [512, 4], P('groups'), parts along dimension 0, may hold values from 0 to 511, as said below
- block_counts: int32 [512], P('groups'), parts along dimension 0, may hold values from 0 to 4, as said below
- shell_norms: float32 [4], replicated, may hold values from 0.5 to 2
Outputs:
- new_vectors: bfloat16 [131072, 256], P(('groups', 'rows', 'cols', 'sub')), parts along dimension 0
- diag_out: float32 [131072], P(('groups', 'rows', 'cols', 'sub')), parts along dimension 0
- next_columns: bfloat16 [131072, 256], P(('groups', 'rows', 'cols', 'sub')), parts along dimension 0
There are 2 independent parts, one for each index of `groups`. A program takes and returns all parts, laid end to end along the dimension named above; an argument that names none is the same for every part. Nothing has to cross between parts.
Inputs may be any that keep to these rules, and one draw needn't show every extreme that they name: `pivots`: 256 distinct AO pairs. `target_blocks`: the used slots of all owners name every block of the 512 blocks exactly once; a used slot's block lies on a device with the owner's cols and sub indices (blocks g * 2 to g * 2 + 1 lie on the device of linear index g, rows slowest; owner o is the device of linear index o). At most 1 of one owner's used slots go to one device, and some owner reaches that in every draw. Entries of unused slots are arbitrary blocks. `block_counts`: some owner uses all 4 slots in every draw.
All inputs are finite; a program needn't handle non-finite values.
Results may differ from a plain program's by a relative error of at most 0.0004.
Values may be sent and summed in bfloat16 or wider, within the bound.
A program may use at most 64 MiB of HBM per device.

v0:
```python
import functools

import jax
import jax.numpy as jnp
from jax import lax
from jax.sharding import PartitionSpec as P


def one_axis_at_a_time(x, axes):
    return functools.reduce(lax.psum, axes, x)


def gathered_total(x, axis):
    return lax.all_gather(x, axis).sum(0)


def slot_plan(row_targets, count, column_size, per_device):
    slot_count = row_targets.shape[0]
    slots = jnp.arange(slot_count, dtype=jnp.int32)
    valid = slots < count
    receiver = row_targets // (column_size * per_device)
    within = row_targets % per_device
    earlier = (
        (receiver[:, None] == receiver[None, :])
        & valid[:, None]
        & valid[None, :]
        & (slots[None, :] < slots[:, None])
    )
    ranking = jnp.sum(earlier.astype(jnp.int32), axis=1)
    return (valid, receiver, ranking, within)


def body(
    stored_vectors,
    previous_columns,
    pivots,
    diagonal,
    ket_blocks,
    shell_tags,
    target_blocks,
    block_counts,
    shell_norms,
):
    rows_here = previous_columns.shape[0]
    batch = previous_columns.shape[1]
    block_rows = ket_blocks.shape[1]
    slot_count = ket_blocks.shape[0]
    per_device = rows_here // block_rows
    band_rows = stored_vectors.shape[1]
    band_index = lax.axis_index("rows")
    device_index = lax.axis_index(("rows", "cols", "sub"))
    column_index = lax.axis_index(("cols", "sub"))
    column_size = lax.axis_size(("cols", "sub"))
    band_size = lax.axis_size("rows")
    peer_slots = (slot_count + band_size - 1) // band_size
    local_pivots = pivots - device_index * rows_here
    matches = jnp.arange(rows_here, dtype=jnp.int32)[:, None] == local_pivots[None, :]
    diag_terms = jnp.sum(jnp.where(matches, diagonal[:, None], jnp.float32(0.0)), axis=0)
    pivot_diag = one_axis_at_a_time(diag_terms, ("rows", "cols", "sub"))
    band_pivots = pivots - band_index * band_rows
    inside = (band_pivots >= 0) & (band_pivots < band_rows)
    clamped = jnp.clip(band_pivots, 0, band_rows - 1)
    taken = jnp.take(stored_vectors, clamped, axis=1).astype(jnp.float32)
    picked = jnp.where(inside[None, :], taken, jnp.float32(0.0))
    pivot_rows = gathered_total(picked, "rows").astype(jnp.bfloat16)
    kinds = jnp.arange(shell_norms.shape[0], dtype=jnp.int32)
    factor = jnp.sum(
        jnp.where(shell_tags[..., None] == kinds, shell_norms, jnp.float32(0.0)), axis=-1
    )
    fresh = (ket_blocks.astype(jnp.float32) * factor[..., None]).astype(jnp.bfloat16)
    own_targets = lax.dynamic_index_in_dim(target_blocks, device_index, 0, keepdims=False)
    own_count = lax.dynamic_index_in_dim(block_counts, device_index, 0, keepdims=False)
    valid, receiver, ranking, within = slot_plan(own_targets, own_count, column_size, per_device)
    lines = jnp.arange(band_size * peer_slots, dtype=jnp.int32)[:, None]
    routing = (
        (lines // peer_slots == receiver[None, :])
        & (lines % peer_slots == ranking[None, :])
        & valid[None, :]
    ).astype(jnp.bfloat16)
    outgoing = jnp.dot(
        routing, fresh.reshape(slot_count, block_rows * batch), preferred_element_type=jnp.float32
    )
    outgoing = outgoing.astype(jnp.bfloat16).reshape(band_size, peer_slots, block_rows, batch)
    incoming = lax.all_to_all(outgoing, "rows", split_axis=0, concat_axis=0, tiled=True)
    sources = jnp.arange(band_size, dtype=jnp.int32) * column_size + column_index
    source_targets = jnp.take(target_blocks, sources, axis=0)
    source_counts = jnp.take(block_counts, sources, axis=0)
    plan_each = jax.vmap(
        lambda row_targets, count: slot_plan(row_targets, count, column_size, per_device)
    )
    source_valid, source_receiver, source_rank, source_within = plan_each(
        source_targets, source_counts
    )
    arriving = source_valid & (source_receiver == band_index)
    places = jnp.arange(per_device, dtype=jnp.int32)[:, None, None, None]
    peer_lines = jnp.arange(peer_slots, dtype=jnp.int32)[None, None, :, None]
    hits = (
        (source_within[None, :, None, :] == places)
        & (source_rank[None, :, None, :] == peer_lines)
        & arriving[None, :, None, :]
    )
    placement = (
        jnp.any(hits, axis=3).astype(jnp.bfloat16).reshape(per_device, band_size * peer_slots)
    )
    arranged = jnp.dot(
        placement,
        incoming.reshape(band_size * peer_slots, block_rows * batch),
        preferred_element_type=jnp.float32,
    )
    next_columns = arranged.astype(jnp.bfloat16).reshape(rows_here, batch)
    product = lax.psum_scatter(
        lax.dot_general(
            stored_vectors, pivot_rows, (((0,), (0,)), ((), ())), preferred_element_type=jnp.float32
        ),
        ("cols", "sub"),
        scatter_dimension=0,
        tiled=True,
    )
    residual_cols = previous_columns.astype(jnp.float32) - product
    scaled = residual_cols / jnp.sqrt(pivot_diag)[None, :]
    new_vectors = scaled.astype(jnp.bfloat16)
    diag_out = diagonal - jnp.sum(scaled * scaled, axis=1)
    return (new_vectors, diag_out, next_columns)


def solution(mesh):
    return jax.shard_map(
        body,
        mesh=mesh,
        in_specs=(
            P(("cols", "sub"), ("groups", "rows")),
            P(("groups", "rows", "cols", "sub"), None),
            P("groups"),
            P(("groups", "rows", "cols", "sub")),
            P(("groups", "rows", "cols", "sub"), None, None),
            P(("groups", "rows", "cols", "sub"), None),
            P("groups", None),
            P("groups"),
            P(),
        ),
        out_specs=(
            P(("groups", "rows", "cols", "sub"), None),
            P(("groups", "rows", "cols", "sub")),
            P(("groups", "rows", "cols", "sub"), None),
        ),
        check_vma=False,
    )
```

profile of v0, /device:TPU:80, one launch (start us, length us, event | category | flops | bytes accessed | tf_op | source)
XLA Modules:
  0.0 233.6 jit_solution(229488856540337576)
XLA Ops:
  7.3 3.2 %copy.43 = bf16[192,4096]{0,1:T(8,128)(2,1)S(1)} copy(bf16[192,4096]{1,0:T(8,128)(2,1)} %param.9) | data formatting | bytes 3145728 | tf_op args[0]
  10.5 1.2 gather_fusion
  11.6 0.1 convert_select_fusion
  11.8 0.8 copy.44
  12.7 110.5 %all-gather.2.cloned.1.call-done = f32[16,192,256]{2,1,0:T(8,128)} async-done(((f32[1,192,256]{2,1,0:T(8,128)}), f32[16,192,256]{2,1,0:T(8,128)}) %all-gather.2.cloned.1.call-update) | async-done | bytes 3145744 | tf_op jit(solution)/shard_map/all_gather | solution.py:14
  123.2 2.1 reduce_sum.54
  125.4 2.6 %convolution_bitcast_fusion = f32[4096,256]{0,1:T(8,128)} fusion(bf16[192,4096]{1,0:T(8,128)(2,1)S(1)} %copy-done.1, bf16[192,256]{0,1:T(8,128)(2,1)S(1)} %copy.50), kind=kOutput, calls=%fused_computation.5 | convolution fusion | flops 402653184 | bytes 5865472 | tf_op jit(solution)/shard_map/dot_general | solution.py:112
  128.1 0.6 copy-done.7
  128.8 0.2 copy-done.2
  129.0 0.1 fusion
  129.1 0.2 copy.51
  129.4 0.6 dynamic_slice.9
  130.0 0.2 dynamic-slice_reduce_fusion
  130.2 0.7 iota_compare_fusion.6
  130.8 0.2 convert_reduce_fusion.1
  131.0 0.4 convolution_convert_fusion
  131.5 1.2 copy.52
  132.7 7.8 %all-to-all-start = ((bf16[16,1,128,256]{3,2,1,0:T(8,128)(2,1)}), bf16[16,1,128,256]{3,2,1,0:T(8,128)(2,1)S(1)}, u32[]{:S(2)}, u32[]{:S(2)}) async-start(bf16[16,1,128,256]{3,2,1,0:T(8,128)(2,1)} %bitcast.5), calls=%async_computation.1 | async-start | bytes 2097152 | tf_op jit(solution)/shard_map/all_to_all | solution.py:84
  140.5 0.1 copy.46
  140.7 0.1 select_reduce_fusion
  140.8 60.8 %psum.21 = f32[256]{0:T(256)S(1)} all-reduce(f32[256]{0:T(256)S(1)} %select_reduce_fusion), channel_id=1, replica_groups=mesh['groups'=2,'rows'=16,'cols'=8,'sub'=2] {'rows'}, use_global_device_ids=true, to_apply=%region_3.4 | all-reduce | flops 256 | bytes 2048 | tf_op jit(solution)/shard_map/psum | solution.py:10
  201.6 17.0 %psum.22 = f32[256]{0:T(256)S(1)} all-reduce(f32[256]{0:T(256)S(1)} %psum.21), channel_id=1, replica_groups=mesh['groups'=2,'rows'=16,'cols'=8,'sub'=2] {'cols'}, use_global_device_ids=true, to_apply=%region_4.5 | all-reduce | flops 256 | bytes 2048 | tf_op jit(solution)/shard_map/psum | solution.py:10
  218.5 2.5 %psum.23 = f32[256]{0:T(256)S(1)} all-reduce(f32[256]{0:T(256)S(1)} %psum.22), channel_id=1, replica_groups=mesh['groups'=2,'rows'=16,'cols'=8,'sub'=2] {'sub'}, use_global_device_ids=true, to_apply=%region_5.6 | all-reduce | flops 256 | bytes 2048 | tf_op jit(solution)/shard_map/psum | solution.py:10
  221.1 0.1 copy.42
  221.2 0.7 gather_fusion.2
  221.9 0.6 gather_fusion.1
  222.7 0.6 copy.53
  223.3 0.3 convolution_convert_fusion.1
  223.6 0.7 reshape.383
  224.3 1.1 multiply_reduce_fusion
  225.4 0.8 copy.49
  226.2 0.6 sub.37
  (41 shorter events, 0.8 us)
Async XLA Ops:
  7.2 3.3 %copy-start.6 = (s32[256]{0:T(256)S(1)}, s32[256]{0:T(256)}, u32[]{:S(2)}) copy-start(s32[256]{0:T(256)} %param.11) | copy-start | bytes 3076
  7.2 116.0 %all-gather.2.cloned.1.call-start = ((), (), s32[]{:S(2)}) async-start(), calls=%async_computation.2 | async-start | bytes 3342336 | tf_op jit(solution)/shard_map/all_gather | solution.py:14
  11.8 113.6 %copy-start.1 = (bf16[192,4096]{1,0:T(8,128)(2,1)S(1)}, bf16[192,4096]{1,0:T(8,128)(2,1)}, u32[]{:S(2)}) copy-start(bf16[192,4096]{1,0:T(8,128)(2,1)} %param.9) | copy-start | bytes 4718596
  12.6 211.7 %reduce-scatter.2.cloned.1.call-start = ((), (), s32[]{:S(2)}) async-start(), calls=%async_computation.3 | async-start | bytes 4456448 | tf_op jit(solution)/shard_map/reduce_scatter | solution.py:111
  128.0 0.7 copy-start.7
  128.0 0.7 copy-start.8
  128.0 1.0 copy-start.2
  128.0 1.3 copy-start
  128.0 1.9 copy-start.4
  131.5 9.2 %copy-start.5 = (f32[256]{0:T(256)S(1)}, f32[256]{0:T(256)}, u32[]{:S(2)}) copy-start(f32[256]{0:T(256)} %param.12) | copy-start | bytes 3076
  131.5 89.6 %copy-start.3 = (bf16[256,256]{1,0:T(8,128)(2,1)S(1)}, bf16[256,256]{1,0:T(8,128)(2,1)}, u32[]{:S(2)}) copy-start(bf16[256,256]{1,0:T(8,128)(2,1)} %param.10) | copy-start | bytes 393220
  132.7 90.0 %all-to-all-start = ((bf16[16,1,128,256]{3,2,1,0:T(8,128)(2,1)}), bf16[16,1,128,256]{3,2,1,0:T(8,128)(2,1)S(1)}, u32[]{:S(2)}, u32[]{:S(2)}) async-start(bf16[16,1,128,256]{3,2,1,0:T(8,128)(2,1)} %bitcast.5), calls=%async_computation.1 | async-start | bytes 2097152 | tf_op jit(solution)/shard_map/all_to_all | solution.py:84
Sparse Core Ops, SparseCore 0:
  12.8 110.3 all-gather.1
  128.2 66.4 reduce-scatter.1
where the time goes:
time: 236 us; the launch traced here: 234 us
  waiting for transfers between devices  111 us (47%)
  blocking collectives  80.3 us (34%)
  between operations  14.3 us (6%)
  local copies, waits for them, and re-layouts  11.7 us (5%)
  starting transfers between devices  7.92 us (3%)
  other arithmetic  5.47 us (2%)
  matrix products  3.34 us (1%)
    all_gather x1, waiting for transfers between devices, gathered_total(): return lax.all_gather(x, axis).sum(0)  110 us
    psum x3, blocking collectives, one_axis_at_a_time(): return functools.reduce(lax.psum, axes, x)  80.3 us
    all_to_all x1, starting transfers between devices, body(): lax.all_to_all(outgoing, 'rows', split_axis=0, concat_axis=0, tiled=True)  7.79 us
    unnamed x26, local copies, waits for them, and re-layouts  7.1 us
  transfers between devices with their start and end apart: 3, of which 1 were waited for; matrix products, arithmetic and copies ran while one was open for 3% of the time, Pallas kernels for 0%

commit v1 on v0

v1 whole, which is shorter than its diff:
```python
import functools

import jax
import jax.numpy as jnp
from jax import lax
from jax.experimental import pallas as pl
from jax.experimental.pallas import tpu as pltpu
from jax.sharding import PartitionSpec as P

MESH = pl.DeviceIdType.MESH
LANES = 128
PIVOT_GROUPS = 4
DIAG_PARTS = 3
BEFORE = 2


def kernel(
    nz,
    nx,
    v_hbm,
    prev_hbm,
    piv_ref,
    diag_ref,
    ket_hbm,
    tags_ref,
    tgt_ref,
    cnt_ref,
    norms_ref,
    new_ref,
    dout_ref,
    next_ref,
    v_ref,
    prev_ref,
    ket_ref,
    fresh_ref,
    hot_ref,
    pick_ref,
    rx1_ref,
    pful_ref,
    snd_ref,
    loc_ref,
    rsib_ref,
    rxr_ref,
    rxl_ref,
    k0_ref,
    krr_ref,
    krl_ref,
    dsnd_ref,
    dsib_ref,
    dsum_ref,
    drx_ref,
    prevt_ref,
    rs_ref,
    outt_ref,
    vsem,
    lsem,
    p1s,
    p1r,
    p2s,
    p2r,
    d2s,
    d2r,
    xrs,
    xrr,
    xls,
    xlr,
    krs,
    krq,
    kls,
    klq,
    dss,
    dsr,
    dxs,
    dxr,
):
    f32, bf16 = jnp.float32, jnp.bfloat16
    depth, band = v_ref.shape
    rows_here, batch = prev_ref.shape
    slots, block_rows = ket_ref.shape[0], ket_ref.shape[1]
    blocks = rows_here // block_rows
    chunk = batch // nz
    per = nz // PIVOT_GROUPS
    grows = per * chunk
    half = nx // 2
    r, c, s = lax.axis_index("rows"), lax.axis_index("cols"), lax.axis_index("sub")
    other = 1 - s
    device = (r * nx + c) * 2 + s
    right, left = lax.rem(c + 1, nx), lax.rem(c + nx - 1, nx)
    up, down = lax.rem(r + 1, nz), lax.rem(r + nz - 1, nz)

    def zpeer(k):
        return lax.rem(r + k, nz)

    def xpeer(k):
        return lax.rem(c + k, nx)

    barrier = pltpu.get_barrier_semaphore()
    by_reach = sorted(range(1, nz), key=lambda k: -min(k, nz - k))
    for k in by_reach:
        pl.semaphore_signal(barrier, inc=1, device_id={"rows": zpeer(k)}, device_id_type=MESH)
    for k in range(1, nx):
        pl.semaphore_signal(barrier, inc=1, device_id={"cols": xpeer(k)}, device_id_type=MESH)
    pl.semaphore_signal(barrier, inc=1, device_id={"sub": other}, device_id_type=MESH)

    pieces = 4
    width = band // pieces
    vload = [
        pltpu.make_async_copy(
            v_hbm.at[:, pl.ds(i * width, width)], v_ref.at[:, pl.ds(i * width, width)], vsem.at[i]
        )
        for i in range(pieces)
    ]
    for copy in vload:
        copy.start()
    ketload = pltpu.make_async_copy(ket_hbm, ket_ref, lsem.at[0])
    ketload.start()
    prevload = pltpu.make_async_copy(prev_hbm, prev_ref, lsem.at[1])
    prevload.start()

    pivot_cols = jnp.transpose(jnp.broadcast_to(piv_ref[...], (LANES, batch)))
    lane = lax.broadcasted_iota(jnp.int32, (batch, LANES), 1)
    in_band = pivot_cols - r * band - lane
    for t in range(band // LANES):
        hot = jnp.where(in_band == t * LANES, f32(1.0), f32(0.0)).astype(bf16)
        hot_ref[:, t * LANES : (t + 1) * LANES] = hot
    in_device = pivot_cols - device * rows_here - lane
    found = jnp.zeros((batch, LANES), f32)
    for t in range(rows_here // LANES):
        row = diag_ref[:, t * LANES : (t + 1) * LANES]
        found = found + jnp.where(in_device == t * LANES, row, f32(0.0))
    own_diag = jnp.sum(found, axis=1, keepdims=True)
    part_hi = own_diag.astype(bf16).astype(f32)
    part_mid = (own_diag - part_hi).astype(bf16).astype(f32)
    part_lo = own_diag - part_hi - part_mid
    spare = pick_ref.shape[1] - depth
    place = lax.broadcasted_iota(jnp.int32, (batch, spare), 1)
    extra = jnp.where(place == 0, part_hi, f32(0.0))
    extra = jnp.where(place == 1, part_mid, extra)
    extra = jnp.where(place == 2, part_lo, extra)
    pick_ref[:, depth:] = extra.astype(bf16)
    picked = jnp.zeros((batch, depth), f32)
    for i in range(pieces):
        vload[i].wait()
        span = slice(i * width, (i + 1) * width)
        picked = picked + lax.dot_general(
            hot_ref[:, span], v_ref[:, span], (((1,), (1,)), ((), ())), preferred_element_type=f32
        )
    pick_ref[:, :depth] = picked.astype(bf16)

    pl.semaphore_wait(barrier, nz - 1 + nx - 1 + 1)

    sends = []

    def push(src, dst, send_sem, recv_sem, to):
        copy = pltpu.make_async_remote_copy(
            src_ref=src,
            dst_ref=dst,
            send_sem=send_sem,
            recv_sem=recv_sem,
            device_id=to,
            device_id_type=MESH,
        )
        copy.start()
        sends.append(copy)

    def arrive(dst, send_sem, recv_sem, to):
        pltpu.make_async_remote_copy(
            src_ref=dst,
            dst_ref=dst,
            send_sem=send_sem,
            recv_sem=recv_sem,
            device_id=to,
            device_id_type=MESH,
        ).wait_recv()

    for k in by_reach:
        to = zpeer(k)
        start = pl.multiple_of(to * chunk, chunk)
        push(
            pick_ref.at[pl.ds(start, chunk), :], rx1_ref.at[k], p1s.at[k], p1r.at[k], {"rows": to}
        )

    ketload.wait()
    tags = tags_ref[...]
    factor = jnp.zeros(tags.shape, f32)
    for kind in range(norms_ref.shape[0]):
        factor = jnp.where(tags == kind, norms_ref[kind], factor)
    for t in range(slots):
        column = jnp.transpose(jnp.broadcast_to(factor[t : t + 1, :], (LANES, block_rows)))
        for h in range(batch // LANES):
            span = slice(h * LANES, (h + 1) * LANES)
            fresh_ref[t, :, span] = (ket_ref[t, :, span].astype(f32) * column).astype(bf16)
    prevload.wait()
    prevt_ref[...] = jnp.transpose(prev_ref[...].astype(f32))

    targets = [jnp.where(t < cnt_ref[device], tgt_ref[t, device], -1) for t in range(slots)]

    def with_own(value, reach, w):
        block = ((lax.rem(r + reach + nz, nz) * nx + c) * 2 + s) * blocks + w
        for t in range(slots):
            value = jnp.where(targets[t] == block, fresh_ref[t], value)
        return value

    zr, zl = nz // 2, nz - 1 - nz // 2

    def ket_right(i):
        if i >= zr:
            return
        for w in range(blocks):
            if i == 0:
                src = k0_ref.at[0, w]
                src[...] = with_own(jnp.zeros(fresh_ref.shape[1:], bf16), zr, w)
            else:
                src = krr_ref.at[i - 1, w]
                arrive(src, krs.at[i - 1, w], krq.at[i - 1, w], {"rows": up})
                src[...] = with_own(src[...], zr - i, w)
            push(src, krr_ref.at[i, w], krs.at[i, w], krq.at[i, w], {"rows": up})

    def ket_left(i):
        if i >= zl:
            return
        for w in range(blocks):
            if i == 0:
                src = k0_ref.at[1, w]
                src[...] = with_own(jnp.zeros(fresh_ref.shape[1:], bf16), -zl, w)
            else:
                src = krl_ref.at[i - 1, w]
                arrive(src, kls.at[i - 1, w], klq.at[i - 1, w], {"rows": down})
                src[...] = with_own(src[...], i - zl, w)
            push(src, krl_ref.at[i, w], kls.at[i, w], klq.at[i, w], {"rows": down})

    def ket(i):
        ket_right(i)
        ket_left(i)

    def ket_last():
        for w in range(blocks):
            arrive(krr_ref.at[zr - 1, w], krs.at[zr - 1, w], krq.at[zr - 1, w], {"rows": up})
            arrive(krl_ref.at[zl - 1, w], kls.at[zl - 1, w], klq.at[zl - 1, w], {"rows": down})
            both = krr_ref[zr - 1, w].astype(f32) + krl_ref[zl - 1, w].astype(f32)
            next_ref[w * block_rows : (w + 1) * block_rows, :] = with_own(both.astype(bf16), 0, w)

    own = pl.multiple_of(r * chunk, chunk)
    total = pick_ref[pl.ds(own, chunk), :].astype(f32)
    for k in range(1, nz):
        arrive(rx1_ref.at[k], p1s.at[k], p1r.at[k], {"rows": zpeer(k)})
        total = total + rx1_ref[k].astype(f32)
    mine = slice(BEFORE * chunk, (BEFORE + 1) * chunk)
    pful_ref[mine, :] = total.astype(bf16)
    for k in reversed(by_reach):
        at = ((BEFORE - k) % nz) * chunk
        push(
            pful_ref.at[mine, :],
            pful_ref.at[pl.ds(at, chunk), :],
            p2s.at[k],
            p2r.at[k],
            {"rows": zpeer(k)},
        )

    order = [(half - p // 2) if p % 2 == 0 else (half + (p + 1) // 2) % nx for p in range(nx)]
    where_is = {rel: p for p, rel in enumerate(order)}
    members = [0, 1, PIVOT_GROUPS - 1] + list(range(2, PIVOT_GROUPS - 1))
    pairs = nx // 2

    def columns_of(p, core):
        rel = order[p]
        return pl.multiple_of((xpeer(rel) * 2 + core) * rows_here, rows_here)

    def multiply(g):
        first = members[g] * per
        for p in range(first, first + per):
            if p != BEFORE:
                k = (BEFORE - p) % nz
                at = pful_ref.at[pl.ds(p * chunk, chunk), :]
                arrive(at, p2s.at[k], p2r.at[k], {"rows": zpeer(k)})
        lhs = pful_ref[first * chunk : first * chunk + grows, :depth]
        for m in range(pairs):
            for p in (2 * m, 2 * m + 1):
                snd_ref[g, p] = jnp.dot(
                    lhs, v_ref[:, pl.ds(columns_of(p, other), rows_here)], preferred_element_type=f32
                )
            span = pl.ds(2 * m, 2)
            push(
                snd_ref.at[g, span], rsib_ref.at[g, span], d2s.at[g, m], d2r.at[g, m], {"sub": other}
            )
        for p in range(nx):
            loc_ref[g, p] = jnp.dot(
                lhs, v_ref[:, pl.ds(columns_of(p, s), rows_here)], preferred_element_type=f32
            )

    met = set()

    def chip_part(g, p):
        m = p // 2
        if (g, m) not in met:
            met.add((g, m))
            arrive(rsib_ref.at[g, pl.ds(2 * m, 2)], d2s.at[g, m], d2r.at[g, m], {"sub": other})
        return loc_ref[g, p] + rsib_ref[g, p]

    def hops(g):
        longer = list(range(half, 0, -1)), list(range(nx - half + 1, nx))
        shorter = list(range(half - 1, 0, -1)), list(range(nx - half, nx))
        return longer if g % 2 == 0 else shorter

    def x_step(g, i):
        for way, (buf, ss, rs, to) in enumerate(
            ((rxr_ref, xrs, xrr, right), (rxl_ref, xls, xlr, left))
        ):
            path = hops(g)[way]
            if i >= len(path):
                continue
            p = where_is[path[i]]
            value = chip_part(g, p)
            if i > 0:
                arrive(buf.at[g, i - 1], ss.at[g, i - 1], rs.at[g, i - 1], {"cols": to})
                value = value + buf[g, i - 1]
            loc_ref[g, p] = value
            push(loc_ref.at[g, p], buf.at[g, i], ss.at[g, i], rs.at[g, i], {"cols": to})

    squares = [jnp.zeros((chunk, rows_here), f32)]

    def finish(g):
        value = chip_part(g, where_is[0])
        for way, (buf, ss, rs, to) in enumerate(
            ((rxr_ref, xrs, xrr, right), (rxl_ref, xls, xlr, left))
        ):
            last = len(hops(g)[way]) - 1
            arrive(buf.at[g, last], ss.at[g, last], rs.at[g, last], {"cols": to})
            value = value + buf[g, last]
        for q in range(per):
            p = members[g] * per + q
            at = pl.multiple_of(lax.rem(p + r + nz - BEFORE, nz) * chunk, chunk)
            scale = rs_ref[p * chunk : (p + 1) * chunk, :]
            scale = jnp.concatenate([scale] * (rows_here // LANES), axis=1)
            scaled = (prevt_ref[pl.ds(at, chunk), :] - value[q * chunk : (q + 1) * chunk]) * scale
            squares[0] = squares[0] + scaled * scaled
            outt_ref[pl.ds(at, chunk), :] = scaled

    def diag_to_sibling():
        tile = depth // LANES
        at = depth - tile * LANES
        turned = jnp.transpose(pful_ref[:, tile * LANES : (tile + 1) * LANES].astype(f32))
        dsnd_ref[...] = (
            turned[at : at + 1, :] + turned[at + 1 : at + 2, :] + turned[at + 2 : at + 3, :]
        )
        push(dsnd_ref, dsib_ref, dss.at[0], dsr.at[0], {"sub": other})

    def diag_to_band():
        arrive(dsib_ref, dss.at[0], dsr.at[0], {"sub": other})
        dsum_ref[...] = dsnd_ref[...] + dsib_ref[...]
        for k in range(1, nx):
            push(dsum_ref, drx_ref.at[k], dxs.at[k], dxr.at[k], {"cols": xpeer(k)})

    def diag_last():
        pivot_diag = dsum_ref[...]
        for k in range(1, nx):
            arrive(drx_ref.at[k], dxs.at[k], dxr.at[k], {"cols": xpeer(k)})
            pivot_diag = pivot_diag + drx_ref[k]
        scale = f32(1.0) / jnp.sqrt(pivot_diag)
        rs_ref[...] = jnp.transpose(jnp.broadcast_to(scale, (LANES, batch)))

    ket(0)
    multiply(0)
    x_step(0, 0)
    ket(1)
    multiply(1)
    x_step(1, 0)
    x_step(0, 1)
    ket(2)
    multiply(2)
    x_step(2, 0)
    x_step(1, 1)
    x_step(0, 2)
    ket(3)
    multiply(3)
    diag_to_sibling()
    x_step(3, 0)
    x_step(2, 1)
    x_step(1, 2)
    x_step(0, 3)
    diag_to_band()
    ket(4)
    x_step(3, 1)
    x_step(2, 2)
    x_step(1, 3)
    diag_last()
    finish(0)
    ket(5)
    x_step(3, 2)
    x_step(2, 3)
    finish(1)
    ket(6)
    x_step(3, 3)
    ket(7)
    finish(2)
    ket_last()
    finish(3)
    new_ref[...] = jnp.transpose(outt_ref[...]).astype(bf16)
    dout_ref[...] = diag_ref[...] - jnp.sum(squares[0], axis=0, keepdims=True)
    for copy in sends:
        copy.wait_send()


def body(
    nz,
    nx,
    stored_vectors,
    previous_columns,
    pivots,
    diagonal,
    ket_blocks,
    shell_tags,
    target_blocks,
    block_counts,
    shell_norms,
):
    depth, band = stored_vectors.shape
    rows_here, batch = previous_columns.shape
    slots, block_rows, _ = ket_blocks.shape
    blocks = rows_here // block_rows
    chunk = batch // nz
    grows = batch // PIVOT_GROUPS
    wide = -(-(depth + DIAG_PARTS) // LANES) * LANES
    zr, zl = nz // 2, nz - 1 - nz // 2
    half = nx // 2
    f32, bf16 = jnp.float32, jnp.bfloat16
    dma = pltpu.SemaphoreType.DMA
    vmem = pl.BlockSpec(memory_space=pltpu.VMEM)
    smem = pl.BlockSpec(memory_space=pltpu.SMEM)
    hbm = pl.BlockSpec(memory_space=pl.ANY)
    new_vectors, diag_out, next_columns = pl.pallas_call(
        functools.partial(kernel, nz, nx),
        out_shape=(
            jax.ShapeDtypeStruct((rows_here, batch), bf16),
            jax.ShapeDtypeStruct((1, rows_here), f32),
            jax.ShapeDtypeStruct((rows_here, batch), bf16),
        ),
        in_specs=[hbm, hbm, vmem, vmem, hbm, vmem, smem, smem, smem],
        out_specs=(vmem, vmem, vmem),
        scratch_shapes=[
            pltpu.VMEM((depth, band), bf16),
            pltpu.VMEM((rows_here, batch), bf16),
            pltpu.VMEM((slots, block_rows, batch), bf16),
            pltpu.VMEM((slots, block_rows, batch), bf16),
            pltpu.VMEM((batch, band), bf16),
            pltpu.VMEM((batch, wide), bf16),
            pltpu.VMEM((nz, chunk, wide), bf16),
            pltpu.VMEM((batch, wide), bf16),
            pltpu.VMEM((PIVOT_GROUPS, nx, grows, rows_here), f32),
            pltpu.VMEM((PIVOT_GROUPS, nx, grows, rows_here), f32),
            pltpu.VMEM((PIVOT_GROUPS, nx, grows, rows_here), f32),
            pltpu.VMEM((PIVOT_GROUPS, half, grows, rows_here), f32),
            pltpu.VMEM((PIVOT_GROUPS, half, grows, rows_here), f32),
            pltpu.VMEM((2, blocks, block_rows, batch), bf16),
            pltpu.VMEM((zr, blocks, block_rows, batch), bf16),
            pltpu.VMEM((zl, blocks, block_rows, batch), bf16),
            pltpu.VMEM((1, batch), f32),
            pltpu.VMEM((1, batch), f32),
            pltpu.VMEM((1, batch), f32),
            pltpu.VMEM((nx, 1, batch), f32),
            pltpu.VMEM((batch, rows_here), f32),
            pltpu.VMEM((batch, LANES), f32),
            pltpu.VMEM((batch, rows_here), f32),
            dma((4,)),
            dma((2,)),
            dma((nz,)),
            dma((nz,)),
            dma((nz,)),
            dma((nz,)),
            dma((PIVOT_GROUPS, half)),
            dma((PIVOT_GROUPS, half)),
            dma((PIVOT_GROUPS, half)),
            dma((PIVOT_GROUPS, half)),
            dma((PIVOT_GROUPS, half)),
            dma((PIVOT_GROUPS, half)),
            dma((zr, blocks)),
            dma((zr, blocks)),
            dma((zl, blocks)),
            dma((zl, blocks)),
            dma((1,)),
            dma((1,)),
            dma((nx,)),
            dma((nx,)),
        ],
        compiler_params=pltpu.CompilerParams(
            collective_id=0, has_side_effects=True, vmem_limit_bytes=48 * 1024 * 1024
        ),
        name="downdate",
    )(
        stored_vectors,
        previous_columns,
        pivots.reshape(1, batch),
        diagonal.reshape(1, rows_here),
        ket_blocks,
        shell_tags,
        target_blocks.T,
        block_counts,
        shell_norms,
    )
    return new_vectors, diag_out.reshape(rows_here), next_columns


def solution(mesh):
    return jax.shard_map(
        functools.partial(body, mesh.shape["rows"], mesh.shape["cols"]),
        mesh=mesh,
        in_specs=(
            P(("cols", "sub"), ("groups", "rows")),
            P(("groups", "rows", "cols", "sub"), None),
            P("groups"),
            P(("groups", "rows", "cols", "sub")),
            P(("groups", "rows", "cols", "sub"), None, None),
            P(("groups", "rows", "cols", "sub"), None),
            P("groups", None),
            P("groups"),
            P(),
        ),
        out_specs=(
            P(("groups", "rows", "cols", "sub"), None),
            P(("groups", "rows", "cols", "sub")),
            P(("groups", "rows", "cols", "sub"), None),
        ),
        check_vma=False,
    )
```

time: 236 us -> 113 us (0.48)
  waiting for transfers between devices: 111 us -> 0 us
  Pallas kernels: 0 us -> 103 us
  blocking collectives: 80.3 us -> 0 us
  between operations: 14.3 us -> 0.66 us
  starting transfers between devices: 7.92 us -> 0 us
  other arithmetic: 5.47 us -> 0 us
  matrix products: 3.34 us -> 0 us
  local copies, waits for them, and re-layouts: 11.7 us -> 9.19 us
    all_gather x1 -> x0, waiting for transfers between devices: 110 us -> none  [gathered_total(): return lax.all_gather(x, axis).sum(0)]
    pallas_call x0 -> x1, Pallas kernels: none -> 103 us  [body(): pl.pallas_call(functools.partial(kernel, nz, nx), out_shape=(jax.ShapeDty...]
    psum x3 -> x0, blocking collectives: 80.3 us -> none  [one_axis_at_a_time(): return functools.reduce(lax.psum, axes, x)]
    all_to_all x1 -> x0, starting transfers between devices: 7.79 us -> none  [body(): lax.all_to_all(outgoing, 'rows', split_axis=0, concat_axis=0, tiled=True)]
    reduce_sum x6 -> x0, other arithmetic: 3.65 us -> none  [the longest x1 2.1 us: gathered_total(): return lax.all_gather(x, axis).sum(0)]
    dot_general x3 -> x0, matrix products: 3.34 us -> none  [the longest x1 2.63 us: body(): lax.dot_general(stored_vectors, pivot_rows, (((0,), (0,)), ((), ())), pre...]
    gather x4 -> x0, local copies, waits for them, and re-layouts: 2.46 us -> none  [the longest x1 1.15 us: body(): taken = jnp.take(stored_vectors, clamped, axis=1).astype(jnp.float32)]
    unnamed x26 -> x21, local copies, waits for them, and re-layouts: 7.1 us -> 9.19 us
  transfers between devices with their start and end apart: 3 -> 0, of which waited for: 1 -> 0; matrix products, arithmetic and copies ran while one was open for 3% -> 0% of each run, Pallas kernels for 0% -> 0%
where the time goes in v1:
time: 113 us
  Pallas kernels  103 us (91%)
  local copies, waits for them, and re-layouts  9.19 us (8%)
    pallas_call x1, Pallas kernels, body(): pl.pallas_call(functools.partial(kernel, nz, nx), out_shape=(jax.ShapeDty...  103 us
    unnamed x21, local copies, waits for them, and re-layouts  9.19 us

profile of v1, /device:TPU:80, one launch (start us, length us, event | category | flops | bytes accessed | tf_op | source)
XLA Modules:
  0.0 112.5 jit_solution(4505964909485838953)
XLA Ops:
  0.6 0.0 copy-start
  0.6 1.4 %copy-done = bf16[192,4096]{1,0:T(8,128)(2,1)S(1)} copy-done((bf16[192,4096]{1,0:T(8,128)(2,1)S(1)}, bf16[192,4096]{1,0:T(8,128)(2,1)}, u32[]{:S(2)}) %copy-start) | copy-done | bytes 1572888
  2.0 0.0 copy-start.1
  2.0 0.9 copy-done.1
  3.0 0.0 copy-start.2
  3.0 0.9 copy-done.2
  3.9 0.0 copy-start.3
  3.9 0.7 copy-done.3
  4.6 0.0 copy-start.4
  4.6 0.7 copy-done.4
  5.3 0.0 copy-start.5
  5.3 0.7 copy-done.5
  5.9 0.0 copy-start.6
  5.9 0.7 copy-done.6
  6.6 0.0 copy-start.7
  6.6 0.7 copy-done.7
  7.3 0.0 copy-start.8
  7.3 0.7 copy-done.8
  8.0 102.7 %downdate.1 = (bf16[256,256]{1,0:T(8,128)(2,1)S(1)}, f32[1,256]{1,0:T(1,128)S(1)}, bf16[256,256]{1,0:T(8,128)(2,1)S(1)}) custom-call(bf16[192,4096]{1,0:T(8,128)(2,1)S(1)} %copy-done, bf16[256,256]{1,0:T(8,128)(2,1)S(1)} %copy-done.2, s32[1,256]{1,0:T(1,128)S(1)} %bitcast.5, f32[1,256]{1,0:T(1,128)S(1)} %bitcast.6, bf16[4,128,256]{2,1,0:T(8,128)(2,1)S(1)} %copy-done.1, ...), custom_call_target="tpu_custom_call" | custom-call | tf_op jit(solution)/shard_map/downdate/pallas_call | solution.py:431
  110.7 0.7 copy.15
  111.3 0.6 copy.16
  111.9 0.7 copy.17
Async XLA Ops:
  0.6 1.4 %copy-start = (bf16[192,4096]{1,0:T(8,128)(2,1)S(1)}, bf16[192,4096]{1,0:T(8,128)(2,1)}, u32[]{:S(2)}) copy-start(bf16[192,4096]{1,0:T(8,128)(2,1)} %v_hbm.1) | copy-start | bytes 4718596
  2.0 0.9 copy-start.1
  3.0 0.9 copy-start.2
  3.9 0.7 copy-start.3
  4.6 0.7 copy-start.4
  5.3 0.7 copy-start.5
  5.9 0.7 copy-start.6
  6.6 0.7 copy-start.7
  7.3 0.7 copy-start.8

commit v2 on v1

--- a/solution.py
+++ b/solution.py
@@ -19,16 +19,25 @@
     nx,
     v_hbm,
     prev_hbm,
+    piv_hbm,
+    diag_hbm,
+    ket_hbm,
+    tags_hbm,
+    tgt_hbm,
+    cnt_hbm,
+    norms_hbm,
+    new_hbm,
+    dout_hbm,
+    next_hbm,
+    new_ref,
+    dout_ref,
+    next_ref,
     piv_ref,
     diag_ref,
-    ket_hbm,
     tags_ref,
     tgt_ref,
     cnt_ref,
     norms_ref,
-    new_ref,
-    dout_ref,
-    next_ref,
     v_ref,
     prev_ref,
     ket_ref,
@@ -72,6 +81,7 @@
     dsr,
     dxs,
     dxr,
+    osem,
 ):
     f32, bf16 = jnp.float32, jnp.bfloat16
     depth, band = v_ref.shape
@@ -94,14 +104,21 @@
     def xpeer(k):
         return lax.rem(c + k, nx)
 
-    barrier = pltpu.get_barrier_semaphore()
-    by_reach = sorted(range(1, nz), key=lambda k: -min(k, nz - k))
-    for k in by_reach:
-        pl.semaphore_signal(barrier, inc=1, device_id={"rows": zpeer(k)}, device_id_type=MESH)
-    for k in range(1, nx):
-        pl.semaphore_signal(barrier, inc=1, device_id={"cols": xpeer(k)}, device_id_type=MESH)
-    pl.semaphore_signal(barrier, inc=1, device_id={"sub": other}, device_id_type=MESH)
-
+    smalls = [
+        pltpu.make_async_copy(src, dst, lsem.at[2 + i])
+        for i, (src, dst) in enumerate(
+            (
+                (piv_hbm, piv_ref),
+                (diag_hbm, diag_ref),
+                (tags_hbm, tags_ref),
+                (tgt_hbm, tgt_ref),
+                (cnt_hbm, cnt_ref),
+                (norms_hbm, norms_ref),
+            )
+        )
+    ]
+    for copy in smalls:
+        copy.start()
     pieces = 4
     width = band // pieces
     vload = [
@@ -117,6 +134,16 @@
     prevload = pltpu.make_async_copy(prev_hbm, prev_ref, lsem.at[1])
     prevload.start()
 
+    barrier = pltpu.get_barrier_semaphore()
+    by_reach = sorted(range(1, nz), key=lambda k: -min(k, nz - k))
+    for k in by_reach:
+        pl.semaphore_signal(barrier, inc=1, device_id={"rows": zpeer(k)}, device_id_type=MESH)
+    for k in range(1, nx):
+        pl.semaphore_signal(barrier, inc=1, device_id={"cols": xpeer(k)}, device_id_type=MESH)
+    pl.semaphore_signal(barrier, inc=1, device_id={"sub": other}, device_id_type=MESH)
+
+    for copy in smalls[:2]:
+        copy.wait()
     pivot_cols = jnp.transpose(jnp.broadcast_to(piv_ref[...], (LANES, batch)))
     lane = lax.broadcasted_iota(jnp.int32, (batch, LANES), 1)
     in_band = pivot_cols - r * band - lane
@@ -149,8 +176,6 @@
 
     pl.semaphore_wait(barrier, nz - 1 + nx - 1 + 1)
 
-    sends = []
-
     def push(src, dst, send_sem, recv_sem, to):
         copy = pltpu.make_async_remote_copy(
             src_ref=src,
@@ -161,26 +186,31 @@
             device_id_type=MESH,
         )
         copy.start()
-        sends.append(copy)
-
-    def arrive(dst, send_sem, recv_sem, to):
-        pltpu.make_async_remote_copy(
-            src_ref=dst,
-            dst_ref=dst,
-            send_sem=send_sem,
-            recv_sem=recv_sem,
+
+    def tally(ref, sem, to, sent=False):
+        copy = pltpu.make_async_remote_copy(
+            src_ref=ref,
+            dst_ref=ref,
+            send_sem=sem,
+            recv_sem=sem,
             device_id=to,
             device_id_type=MESH,
-        ).wait_recv()
+        )
+        if sent:
+            copy.wait_send()
+        else:
+            copy.wait_recv()
 
     for k in by_reach:
         to = zpeer(k)
         start = pl.multiple_of(to * chunk, chunk)
         push(
-            pick_ref.at[pl.ds(start, chunk), :], rx1_ref.at[k], p1s.at[k], p1r.at[k], {"rows": to}
+            pick_ref.at[pl.ds(start, chunk), :], rx1_ref.at[k - 1], p1s.at[0], p1r.at[0], {"rows": to}
         )
 
     ketload.wait()
+    for copy in smalls[2:]:
+        copy.wait()
     tags = tags_ref[...]
     factor = jnp.zeros(tags.shape, f32)
     for kind in range(norms_ref.shape[0]):
@@ -212,9 +242,9 @@
                 src[...] = with_own(jnp.zeros(fresh_ref.shape[1:], bf16), zr, w)
             else:
                 src = krr_ref.at[i - 1, w]
-                arrive(src, krs.at[i - 1, w], krq.at[i - 1, w], {"rows": up})
+                tally(src, krq.at[i - 1, w], {"rows": up})
                 src[...] = with_own(src[...], zr - i, w)
-            push(src, krr_ref.at[i, w], krs.at[i, w], krq.at[i, w], {"rows": up})
+            push(src, krr_ref.at[i, w], krs.at[0], krq.at[i, w], {"rows": up})
 
     def ket_left(i):
         if i >= zl:
@@ -225,9 +255,9 @@
                 src[...] = with_own(jnp.zeros(fresh_ref.shape[1:], bf16), -zl, w)
             else:
                 src = krl_ref.at[i - 1, w]
-                arrive(src, kls.at[i - 1, w], klq.at[i - 1, w], {"rows": down})
+                tally(src, klq.at[i - 1, w], {"rows": down})
                 src[...] = with_own(src[...], i - zl, w)
-            push(src, krl_ref.at[i, w], kls.at[i, w], klq.at[i, w], {"rows": down})
+            push(src, krl_ref.at[i, w], kls.at[0], klq.at[i, w], {"rows": down})
 
     def ket(i):
         ket_right(i)
@@ -235,28 +265,33 @@
 
     def ket_last():
         for w in range(blocks):
-            arrive(krr_ref.at[zr - 1, w], krs.at[zr - 1, w], krq.at[zr - 1, w], {"rows": up})
-            arrive(krl_ref.at[zl - 1, w], kls.at[zl - 1, w], klq.at[zl - 1, w], {"rows": down})
+            tally(krr_ref.at[zr - 1, w], krq.at[zr - 1, w], {"rows": up})
+            tally(krl_ref.at[zl - 1, w], klq.at[zl - 1, w], {"rows": down})
             both = krr_ref[zr - 1, w].astype(f32) + krl_ref[zl - 1, w].astype(f32)
             next_ref[w * block_rows : (w + 1) * block_rows, :] = with_own(both.astype(bf16), 0, w)
 
+    ket(0)
+
+    def broadcast():
+        for k in reversed(by_reach):
+            at = ((BEFORE - k) % nz) * chunk
+            push(
+                pful_ref.at[mine, :],
+                pful_ref.at[pl.ds(at, chunk), :],
+                p2s.at[0],
+                p2r.at[((BEFORE - k) % nz) // per],
+                {"rows": zpeer(k)},
+            )
+
+    mine = slice(BEFORE * chunk, (BEFORE + 1) * chunk)
+
     own = pl.multiple_of(r * chunk, chunk)
     total = pick_ref[pl.ds(own, chunk), :].astype(f32)
+    tally(rx1_ref, p1r.at[0], {"rows": up})
     for k in range(1, nz):
-        arrive(rx1_ref.at[k], p1s.at[k], p1r.at[k], {"rows": zpeer(k)})
-        total = total + rx1_ref[k].astype(f32)
-    mine = slice(BEFORE * chunk, (BEFORE + 1) * chunk)
+        total = total + rx1_ref[k - 1].astype(f32)
     pful_ref[mine, :] = total.astype(bf16)
-    for k in reversed(by_reach):
-        at = ((BEFORE - k) % nz) * chunk
-        push(
-            pful_ref.at[mine, :],
-            pful_ref.at[pl.ds(at, chunk), :],
-            p2s.at[k],
-            p2r.at[k],
-            {"rows": zpeer(k)},
-        )
-
+    broadcast()
     order = [(half - p // 2) if p % 2 == 0 else (half + (p + 1) // 2) % nx for p in range(nx)]
     where_is = {rel: p for p, rel in enumerate(order)}
     members = [0, 1, PIVOT_GROUPS - 1] + list(range(2, PIVOT_GROUPS - 1))
@@ -268,11 +303,8 @@
 
     def multiply(g):
         first = members[g] * per
-        for p in range(first, first + per):
-            if p != BEFORE:
-                k = (BEFORE - p) % nz
-                at = pful_ref.at[pl.ds(p * chunk, chunk), :]
-                arrive(at, p2s.at[k], p2r.at[k], {"rows": zpeer(k)})
+        coming = per - (1 if first <= BEFORE < first + per else 0)
+        tally(pful_ref.at[pl.ds(0, coming * chunk), :], p2r.at[members[g]], {"rows": up})
         lhs = pful_ref[first * chunk : first * chunk + grows, :depth]
         for m in range(pairs):
             for p in (2 * m, 2 * m + 1):
@@ -281,7 +313,7 @@
                 )
             span = pl.ds(2 * m, 2)
             push(
-                snd_ref.at[g, span], rsib_ref.at[g, span], d2s.at[g, m], d2r.at[g, m], {"sub": other}
+                snd_ref.at[g, span], rsib_ref.at[g, span], d2s.at[0], d2r.at[g, m], {"sub": other}
             )
         for p in range(nx):
             loc_ref[g, p] = jnp.dot(
@@ -294,13 +326,16 @@
         m = p // 2
         if (g, m) not in met:
             met.add((g, m))
-            arrive(rsib_ref.at[g, pl.ds(2 * m, 2)], d2s.at[g, m], d2r.at[g, m], {"sub": other})
+            tally(rsib_ref.at[g, pl.ds(2 * m, 2)], d2r.at[g, m], {"sub": other})
         return loc_ref[g, p] + rsib_ref[g, p]
 
     def hops(g):
         longer = list(range(half, 0, -1)), list(range(nx - half + 1, nx))
         shorter = list(range(half - 1, 0, -1)), list(range(nx - half, nx))
         return longer if g % 2 == 0 else shorter
+
+    def spot(g, way, i):
+        return sum(len(hops(q)[way]) for q in range(g)) + i
 
     def x_step(g, i):
         for way, (buf, ss, rs, to) in enumerate(
@@ -312,10 +347,12 @@
             p = where_is[path[i]]
             value = chip_part(g, p)
             if i > 0:
-                arrive(buf.at[g, i - 1], ss.at[g, i - 1], rs.at[g, i - 1], {"cols": to})
-                value = value + buf[g, i - 1]
+                came = spot(g, way, i - 1)
+                tally(buf.at[came], rs.at[came], {"cols": to})
+                value = value + buf[came]
             loc_ref[g, p] = value
-            push(loc_ref.at[g, p], buf.at[g, i], ss.at[g, i], rs.at[g, i], {"cols": to})
+            goes = spot(g, way, i)
+            push(loc_ref.at[g, p], buf.at[goes], ss.at[0], rs.at[goes], {"cols": to})
 
     squares = [jnp.zeros((chunk, rows_here), f32)]
 
@@ -324,9 +361,9 @@
         for way, (buf, ss, rs, to) in enumerate(
             ((rxr_ref, xrs, xrr, right), (rxl_ref, xls, xlr, left))
         ):
-            last = len(hops(g)[way]) - 1
-            arrive(buf.at[g, last], ss.at[g, last], rs.at[g, last], {"cols": to})
-            value = value + buf[g, last]
+            last = spot(g, way, len(hops(g)[way]) - 1)
+            tally(buf.at[last], rs.at[last], {"cols": to})
+            value = value + buf[last]
         for q in range(per):
             p = members[g] * per + q
             at = pl.multiple_of(lax.rem(p + r + nz - BEFORE, nz) * chunk, chunk)
@@ -346,50 +383,49 @@
         push(dsnd_ref, dsib_ref, dss.at[0], dsr.at[0], {"sub": other})
 
     def diag_to_band():
-        arrive(dsib_ref, dss.at[0], dsr.at[0], {"sub": other})
+        tally(dsib_ref, dsr.at[0], {"sub": other})
         dsum_ref[...] = dsnd_ref[...] + dsib_ref[...]
         for k in range(1, nx):
-            push(dsum_ref, drx_ref.at[k], dxs.at[k], dxr.at[k], {"cols": xpeer(k)})
+            push(dsum_ref, drx_ref.at[k - 1], dxs.at[0], dxr.at[0], {"cols": xpeer(k)})
 
     def diag_last():
         pivot_diag = dsum_ref[...]
+        tally(drx_ref, dxr.at[0], {"cols": right})
         for k in range(1, nx):
-            arrive(drx_ref.at[k], dxs.at[k], dxr.at[k], {"cols": xpeer(k)})
-            pivot_diag = pivot_diag + drx_ref[k]
+            pivot_diag = pivot_diag + drx_ref[k - 1]
         scale = f32(1.0) / jnp.sqrt(pivot_diag)
         rs_ref[...] = jnp.transpose(jnp.broadcast_to(scale, (LANES, batch)))
 
-    ket(0)
+    ket(1)
     multiply(0)
     x_step(0, 0)
-    ket(1)
     multiply(1)
     x_step(1, 0)
+    ket(2)
     x_step(0, 1)
-    ket(2)
     multiply(2)
     x_step(2, 0)
     x_step(1, 1)
+    ket(3)
     x_step(0, 2)
-    ket(3)
     multiply(3)
     diag_to_sibling()
     x_step(3, 0)
     x_step(2, 1)
+    ket(4)
     x_step(1, 2)
     x_step(0, 3)
     diag_to_band()
-    ket(4)
     x_step(3, 1)
     x_step(2, 2)
+    ket(5)
     x_step(1, 3)
     diag_last()
     finish(0)
-    ket(5)
     x_step(3, 2)
     x_step(2, 3)
+    ket(6)
     finish(1)
-    ket(6)
     x_step(3, 3)
     ket(7)
     finish(2)
@@ -397,8 +433,28 @@
     finish(3)
     new_ref[...] = jnp.transpose(outt_ref[...]).astype(bf16)
     dout_ref[...] = diag_ref[...] - jnp.sum(squares[0], axis=0, keepdims=True)
-    for copy in sends:
-        copy.wait_send()
+    outs = [
+        pltpu.make_async_copy(src, dst, osem.at[i])
+        for i, (src, dst) in enumerate(
+            ((new_ref, new_hbm), (dout_ref, dout_hbm), (next_ref, next_hbm))
+        )
+    ]
+    for copy in outs:
+        copy.start()
+    for ref, sem, to in (
+        (rx1_ref, p1s, {"rows": up}),
+        (rx1_ref, p2s, {"rows": up}),
+        (rsib_ref, d2s, {"sub": other}),
+        (rxr_ref, xrs, {"cols": right}),
+        (rxl_ref, xls, {"cols": left}),
+        (krr_ref, krs, {"rows": up}),
+        (krl_ref, kls, {"rows": down}),
+        (dsib_ref, dss, {"sub": other}),
+        (drx_ref, dxs, {"cols": right}),
+    ):
+        tally(ref, sem.at[0], to, sent=True)
+    for copy in outs:
+        copy.wait()
 
 
 def body(
@@ -423,11 +479,11 @@
     wide = -(-(depth + DIAG_PARTS) // LANES) * LANES
     zr, zl = nz // 2, nz - 1 - nz // 2
     half = nx // 2
+    x_messages = PIVOT_GROUPS * (nx - 1) // 2
     f32, bf16 = jnp.float32, jnp.bfloat16
     dma = pltpu.SemaphoreType.DMA
     vmem = pl.BlockSpec(memory_space=pltpu.VMEM)
-    smem = pl.BlockSpec(memory_space=pltpu.SMEM)
-    hbm = pl.BlockSpec(memory_space=pl.ANY)
+    hbm = pl.BlockSpec(memory_space=pltpu.HBM)
     new_vectors, diag_out, next_columns = pl.pallas_call(
         functools.partial(kernel, nz, nx),
         out_shape=(
@@ -435,55 +491,65 @@
             jax.ShapeDtypeStruct((1, rows_here), f32),
             jax.ShapeDtypeStruct((rows_here, batch), bf16),
         ),
-        in_specs=[hbm, hbm, vmem, vmem, hbm, vmem, smem, smem, smem],
-        out_specs=(vmem, vmem, vmem),
+        in_specs=[hbm] * 9,
+        out_specs=(hbm, hbm, hbm),
         scratch_shapes=[
+            pltpu.VMEM((rows_here, batch), bf16),
+            pltpu.VMEM((1, rows_here), f32),
+            pltpu.VMEM((rows_here, batch), bf16),
+            pltpu.VMEM((1, batch), jnp.int32),
+            pltpu.VMEM((1, rows_here), f32),
+            pltpu.VMEM((slots, block_rows), jnp.int32),
+            pltpu.SMEM(target_blocks.shape[::-1], jnp.int32),
+            pltpu.SMEM(block_counts.shape, jnp.int32),
+            pltpu.SMEM(shell_norms.shape, f32),
             pltpu.VMEM((depth, band), bf16),
             pltpu.VMEM((rows_here, batch), bf16),
             pltpu.VMEM((slots, block_rows, batch), bf16),
             pltpu.VMEM((slots, block_rows, batch), bf16),
             pltpu.VMEM((batch, band), bf16),
             pltpu.VMEM((batch, wide), bf16),
-            pltpu.VMEM((nz, chunk, wide), bf16),
+            pltpu.VMEM((nz - 1, chunk, wide), bf16),
             pltpu.VMEM((batch, wide), bf16),
             pltpu.VMEM((PIVOT_GROUPS, nx, grows, rows_here), f32),
             pltpu.VMEM((PIVOT_GROUPS, nx, grows, rows_here), f32),
             pltpu.VMEM((PIVOT_GROUPS, nx, grows, rows_here), f32),
-            pltpu.VMEM((PIVOT_GROUPS, half, grows, rows_here), f32),
-            pltpu.VMEM((PIVOT_GROUPS, half, grows, rows_here), f32),
+            pltpu.VMEM((x_messages, grows, rows_here), f32),
+            pltpu.VMEM((x_messages, grows, rows_here), f32),
             pltpu.VMEM((2, blocks, block_rows, batch), bf16),
             pltpu.VMEM((zr, blocks, block_rows, batch), bf16),
             pltpu.VMEM((zl, blocks, block_rows, batch), bf16),
             pltpu.VMEM((1, batch), f32),
             pltpu.VMEM((1, batch), f32),
             pltpu.VMEM((1, batch), f32),
-            pltpu.VMEM((nx, 1, batch), f32),
+            pltpu.VMEM((nx - 1, 1, batch), f32),
             pltpu.VMEM((batch, rows_here), f32),
             pltpu.VMEM((batch, LANES), f32),
             pltpu.VMEM((batch, rows_here), f32),
             dma((4,)),
-            dma((2,)),
-            dma((nz,)),
-            dma((nz,)),
-            dma((nz,)),
-            dma((nz,)),
+            dma((8,)),
+            dma((1,)),
+            dma((1,)),
+            dma((1,)),
+            dma((PIVOT_GROUPS,)),
+            dma((1,)),
             dma((PIVOT_GROUPS, half)),
-            dma((PIVOT_GROUPS, half)),
-            dma((PIVOT_GROUPS, half)),
-            dma((PIVOT_GROUPS, half)),
-            dma((PIVOT_GROUPS, half)),
-            dma((PIVOT_GROUPS, half)),
+            dma((1,)),
+            dma((x_messages,)),
+            dma((1,)),
+            dma((x_messages,)),
+            dma((1,)),
             dma((zr, blocks)),
-            dma((zr, blocks)),
+            dma((1,)),
             dma((zl, blocks)),
-            dma((zl, blocks)),
-            dma((1,)),
-            dma((1,)),
-            dma((nx,)),
-            dma((nx,)),
+            dma((1,)),
+            dma((1,)),
+            dma((1,)),
+            dma((1,)),
+            dma((3,)),
         ],
         compiler_params=pltpu.CompilerParams(
-            collective_id=0, has_side_effects=True, vmem_limit_bytes=48 * 1024 * 1024
+            collective_id=0, has_side_effects=True, vmem_limit_bytes=67043328
         ),
         name="downdate",
     )(

time: 113 us -> 101 us (0.89)
  Pallas kernels: 103 us -> 95.5 us
  local copies, waits for them, and re-layouts: 9.19 us -> 4.37 us
    pallas_call x1, Pallas kernels: 103 us -> 95.5 us  [body(): pl.pallas_call(functools.partial(kernel, nz, nx), out_shape=(jax.ShapeDty...]
    unnamed x21 -> x3, local copies, waits for them, and re-layouts: 9.19 us -> 4.37 us
where the time goes in v2:
time: 101 us; the launch traced here: 100 us
  Pallas kernels  95.5 us (95%)
  local copies, waits for them, and re-layouts  4.37 us (4%)
    pallas_call x1, Pallas kernels, body(): pl.pallas_call(functools.partial(kernel, nz, nx), out_shape=(jax.ShapeDty...  95.5 us
    unnamed x3, local copies, waits for them, and re-layouts  4.37 us

profile of v2, /device:TPU:80, one launch (start us, length us, event | category | flops | bytes accessed | tf_op | source)
XLA Modules:
  0.0 100.5 jit_solution(10133483272723333234)
XLA Ops:
  0.6 95.5 %downdate.1 = (bf16[256,256]{1,0:T(8,128)(2,1)}, f32[1,256]{1,0:T(1,128)}, bf16[256,256]{1,0:T(8,128)(2,1)}) custom-call(bf16[192,4096]{1,0:T(8,128)(2,1)} %v_hbm.1, bf16[256,256]{1,0:T(8,128)(2,1)} %prev_hbm.1, s32[1,256]{1,0:T(1,128)} %bitcast.5, f32[1,256]{1,0:T(1,128)} %bitcast.6, bf16[4,128,256]{2,1,0:T(8,128)(2,1)} %ket_hbm.1, s32[4,128]{1,0:T(4,128)} %tags_hbm.1, ...), custom_call_target="tpu_custom_call" | custom-call | tf_op jit(solution)/shard_map/downdate/pallas_call | solution.py:487
  96.1 1.6 %copy.15 = bf16[256,256]{1,0:T(8,128)(2,1)} copy(bf16[256,256]{1,0:T(8,128)(2,1)} %get-tuple-element.12) | data formatting | bytes 262144
  97.7 1.2 %copy.16 = f32[256]{0:T(256)} copy(f32[256]{0:T(256)} %bitcast.7) | data formatting | bytes 2048
  98.9 1.6 %copy.17 = bf16[256,256]{1,0:T(8,128)(2,1)} copy(bf16[256,256]{1,0:T(8,128)(2,1)} %get-tuple-element.14) | data formatting | bytes 262144

commit v3 on v2

--- a/solution.py
+++ b/solution.py
@@ -26,9 +26,6 @@
     tgt_hbm,
     cnt_hbm,
     norms_hbm,
-    new_hbm,
-    dout_hbm,
-    next_hbm,
     new_ref,
     dout_ref,
     next_ref,
@@ -81,7 +78,6 @@
     dsr,
     dxs,
     dxr,
-    osem,
 ):
     f32, bf16 = jnp.float32, jnp.bfloat16
     depth, band = v_ref.shape
@@ -433,14 +429,6 @@
     finish(3)
     new_ref[...] = jnp.transpose(outt_ref[...]).astype(bf16)
     dout_ref[...] = diag_ref[...] - jnp.sum(squares[0], axis=0, keepdims=True)
-    outs = [
-        pltpu.make_async_copy(src, dst, osem.at[i])
-        for i, (src, dst) in enumerate(
-            ((new_ref, new_hbm), (dout_ref, dout_hbm), (next_ref, next_hbm))
-        )
-    ]
-    for copy in outs:
-        copy.start()
     for ref, sem, to in (
         (rx1_ref, p1s, {"rows": up}),
         (rx1_ref, p2s, {"rows": up}),
@@ -453,7 +441,18 @@
         (drx_ref, dxs, {"cols": right}),
     ):
         tally(ref, sem.at[0], to, sent=True)
-    for copy in outs:
+
+
+def write_out(new_ref, dout_ref, next_ref, new_hbm, dout_hbm, next_hbm, sem):
+    copies = [
+        pltpu.make_async_copy(src, dst, sem.at[i])
+        for i, (src, dst) in enumerate(
+            ((new_ref, new_hbm), (next_ref, next_hbm), (dout_ref, dout_hbm))
+        )
+    ]
+    for copy in copies:
+        copy.start()
+    for copy in copies:
         copy.wait()
 
 
@@ -484,19 +483,16 @@
     dma = pltpu.SemaphoreType.DMA
     vmem = pl.BlockSpec(memory_space=pltpu.VMEM)
     hbm = pl.BlockSpec(memory_space=pltpu.HBM)
-    new_vectors, diag_out, next_columns = pl.pallas_call(
+    results = pl.pallas_call(
         functools.partial(kernel, nz, nx),
         out_shape=(
-            jax.ShapeDtypeStruct((rows_here, batch), bf16),
-            jax.ShapeDtypeStruct((1, rows_here), f32),
-            jax.ShapeDtypeStruct((rows_here, batch), bf16),
-        ),
-        in_specs=[hbm] * 9,
-        out_specs=(hbm, hbm, hbm),
-        scratch_shapes=[
             pltpu.VMEM((rows_here, batch), bf16),
             pltpu.VMEM((1, rows_here), f32),
             pltpu.VMEM((rows_here, batch), bf16),
+        ),
+        in_specs=[hbm] * 9,
+        out_specs=(vmem, vmem, vmem),
+        scratch_shapes=[
             pltpu.VMEM((1, batch), jnp.int32),
             pltpu.VMEM((1, rows_here), f32),
             pltpu.VMEM((slots, block_rows), jnp.int32),
@@ -546,23 +542,39 @@
             dma((1,)),
             dma((1,)),
             dma((1,)),
-            dma((3,)),
         ],
         compiler_params=pltpu.CompilerParams(
-            collective_id=0, has_side_effects=True, vmem_limit_bytes=67043328
+            collective_id=0, has_side_effects=True, vmem_limit_bytes=24 * 1024 * 1024
         ),
         name="downdate",
     )(
-        stored_vectors,
-        previous_columns,
-        pivots.reshape(1, batch),
-        diagonal.reshape(1, rows_here),
-        ket_blocks,
-        shell_tags,
-        target_blocks.T,
-        block_counts,
-        shell_norms,
+        *(
+            pltpu.with_memory_space_constraint(x, pltpu.HBM)
+            for x in (
+                stored_vectors,
+                previous_columns,
+                pivots.reshape(1, batch),
+                diagonal.reshape(1, rows_here),
+                ket_blocks,
+                shell_tags,
+                target_blocks.T,
+                block_counts,
+                shell_norms,
+            )
+        )
     )
+    new_vectors, diag_out, next_columns = pl.pallas_call(
+        write_out,
+        out_shape=(
+            pltpu.HBM((rows_here, batch), bf16),
+            pltpu.HBM((1, rows_here), f32),
+            pltpu.HBM((rows_here, batch), bf16),
+        ),
+        in_specs=[vmem] * 3,
+        out_specs=(hbm, hbm, hbm),
+        scratch_shapes=[dma((3,))],
+        name="write_out",
+    )(*(pltpu.with_memory_space_constraint(x, pltpu.VMEM) for x in results))
     return new_vectors, diag_out.reshape(rows_here), next_columns
 
 

time: 101 us -> 96.3 us (0.953)
  local copies, waits for them, and re-layouts: 4.37 us -> 0 us
    unnamed x3 -> x0, local copies, waits for them, and re-layouts: 4.37 us -> none
    pallas_call x1 -> x2, Pallas kernels: 95.5 us -> 95.6 us  [the longest x1 94.8 us: body(): pl.pallas_call(functools.partial(kernel, nz, nx), out_shape=(pltpu.VMEM((...]
where the time goes in v3:
time: 96.3 us; the launch traced here: 96.2 us
  Pallas kernels  95.6 us (99%)
    pallas_call x1, Pallas kernels, body(): pl.pallas_call(functools.partial(kernel, nz, nx), out_shape=(pltpu.VMEM((...  94.8 us

profile of v3, /device:TPU:80, one launch (start us, length us, event | category | flops | bytes accessed | tf_op | source)
XLA Modules:
  0.0 96.2 jit_solution(10671530270788820998)
XLA Ops:
  0.6 94.8 %downdate.1 = (bf16[256,256]{1,0:T(8,128)(2,1)S(1)}, f32[1,256]{1,0:T(1,128)S(1)}, bf16[256,256]{1,0:T(8,128)(2,1)S(1)}) custom-call(bf16[192,4096]{1,0:T(8,128)(2,1)} %v_hbm.1, bf16[256,256]{1,0:T(8,128)(2,1)} %prev_hbm.1, s32[1,256]{1,0:T(1,128)} %bitcast.5, f32[1,256]{1,0:T(1,128)} %bitcast.6, bf16[4,128,256]{2,1,0:T(8,128)(2,1)} %ket_hbm.1, ...), custom_call_target="tpu_custom_call" | custom-call | tf_op jit(solution)/shard_map/downdate/pallas_call | solution.py:486
  95.5 0.7 write_out.1

commit v4 on v3

--- a/solution.py
+++ b/solution.py
@@ -49,6 +49,7 @@
     rxr_ref,
     rxl_ref,
     k0_ref,
+    n1_ref,
     krr_ref,
     krl_ref,
     dsnd_ref,
@@ -223,61 +224,87 @@
 
     def with_own(value, reach, w):
         block = ((lax.rem(r + reach + nz, nz) * nx + c) * 2 + s) * blocks + w
-        for t in range(slots):
-            value = jnp.where(targets[t] == block, fresh_ref[t], value)
-        return value
+        slot, hit = 0, targets[0] == block
+        for t in range(1, slots):
+            slot = jnp.where(targets[t] == block, t, slot)
+            hit = hit | (targets[t] == block)
+        return jnp.where(hit, fresh_ref[slot], value)
 
     zr, zl = nz // 2, nz - 1 - nz // 2
 
-    def ket_right(i):
-        if i >= zr:
+    def chain(i, way):
+        last, buf, stage, ss, rs, k = (
+            (zr, krr_ref, 0, krs, krq, 1) if way > 0 else (zl, krl_ref, 1, kls, klq, nz - 1)
+        )
+        if i >= last:
             return
+        to = {"rows": zpeer(k)}
+        reach = way * (last - i)
+        if i == 0:
+            src = k0_ref.at[stage, 0]
+            value = jnp.zeros(fresh_ref.shape[1:], bf16)
+            for w in range(blocks):
+                value = with_own(value, reach, w)
+            src[...] = value
+            push(src, buf.at[0], ss.at[0], rs.at[0], to)
+            return
+        if i == 1:
+            tally(buf.at[0], rs.at[0], to)
+            first = buf[0]
+            before = (zpeer(nz - k) * nx + c) * 2 + s
+            theirs = [
+                jnp.where(t < cnt_ref[before], tgt_ref[t, before], -1) for t in range(slots)
+            ]
         for w in range(blocks):
-            if i == 0:
-                src = k0_ref.at[0, w]
-                src[...] = with_own(jnp.zeros(fresh_ref.shape[1:], bf16), zr, w)
+            goes = 1 + (i - 1) * blocks + w
+            if i == 1:
+                block = ((lax.rem(r + reach + nz, nz) * nx + c) * 2 + s) * blocks + w
+                value = jnp.zeros(fresh_ref.shape[1:], bf16)
+                for t in range(slots):
+                    value = jnp.where(theirs[t] == block, first, value)
+                src = n1_ref.at[stage, w]
             else:
-                src = krr_ref.at[i - 1, w]
-                tally(src, krq.at[i - 1, w], {"rows": up})
-                src[...] = with_own(src[...], zr - i, w)
-            push(src, krr_ref.at[i, w], krs.at[0], krq.at[i, w], {"rows": up})
-
-    def ket_left(i):
-        if i >= zl:
-            return
-        for w in range(blocks):
-            if i == 0:
-                src = k0_ref.at[1, w]
-                src[...] = with_own(jnp.zeros(fresh_ref.shape[1:], bf16), -zl, w)
-            else:
-                src = krl_ref.at[i - 1, w]
-                tally(src, klq.at[i - 1, w], {"rows": down})
-                src[...] = with_own(src[...], i - zl, w)
-            push(src, krl_ref.at[i, w], kls.at[0], klq.at[i, w], {"rows": down})
+                src = buf.at[goes - blocks]
+                tally(src, rs.at[goes - blocks], to)
+                value = src[...]
+            src[...] = with_own(value, reach, w)
+            push(src, buf.at[goes], ss.at[0], rs.at[goes], to)
 
     def ket(i):
-        ket_right(i)
-        ket_left(i)
+        chain(i, 1)
+        chain(i, -1)
 
     def ket_last():
         for w in range(blocks):
-            tally(krr_ref.at[zr - 1, w], krq.at[zr - 1, w], {"rows": up})
-            tally(krl_ref.at[zl - 1, w], klq.at[zl - 1, w], {"rows": down})
-            both = krr_ref[zr - 1, w].astype(f32) + krl_ref[zl - 1, w].astype(f32)
+            end_r, end_l = 1 + (zr - 2) * blocks + w, 1 + (zl - 2) * blocks + w
+            tally(krr_ref.at[end_r], krq.at[end_r], {"rows": up})
+            tally(krl_ref.at[end_l], klq.at[end_l], {"rows": down})
+            both = krr_ref[end_r].astype(f32) + krl_ref[end_l].astype(f32)
             next_ref[w * block_rows : (w + 1) * block_rows, :] = with_own(both.astype(bf16), 0, w)
 
     ket(0)
+    ket(1)
+
+    quarter = nz // 4
+
+    def pass_on(src, k, to):
+        p = (BEFORE - k) % nz
+        sem = PIVOT_GROUPS + (1 if k == quarter else 0) if k in (quarter, nz - quarter) else p // per
+        push(src, pful_ref.at[pl.ds(p * chunk, chunk), :], p2s.at[0], p2r.at[sem], {"rows": to})
 
     def broadcast():
         for k in reversed(by_reach):
-            at = ((BEFORE - k) % nz) * chunk
-            push(
-                pful_ref.at[mine, :],
-                pful_ref.at[pl.ds(at, chunk), :],
-                p2s.at[0],
-                p2r.at[((BEFORE - k) % nz) // per],
-                {"rows": zpeer(k)},
-            )
+            if min(k, nz - k) <= quarter:
+                pass_on(pful_ref.at[mine, :], k, zpeer(k))
+
+    def relay():
+        for i, (k, hops_on) in enumerate(
+            ((nz - quarter, range(-1, -quarter, -1)), (quarter, range(1, quarter + 1)))
+        ):
+            held = pful_ref.at[pl.ds(((BEFORE - k) % nz) * chunk, chunk), :]
+            tally(held, p2r.at[PIVOT_GROUPS + i], {"rows": up})
+            for hop in hops_on:
+                pass_on(held, (k + hop) % nz, zpeer(hop % nz))
 
     mine = slice(BEFORE * chunk, (BEFORE + 1) * chunk)
 
@@ -299,7 +326,8 @@
 
     def multiply(g):
         first = members[g] * per
-        coming = per - (1 if first <= BEFORE < first + per else 0)
+        known = (BEFORE, (BEFORE - quarter) % nz, (BEFORE + quarter) % nz)
+        coming = per - sum(first <= p < first + per for p in known)
         tally(pful_ref.at[pl.ds(0, coming * chunk), :], p2r.at[members[g]], {"rows": up})
         lhs = pful_ref[first * chunk : first * chunk + grows, :depth]
         for m in range(pairs):
@@ -392,38 +420,39 @@
         scale = f32(1.0) / jnp.sqrt(pivot_diag)
         rs_ref[...] = jnp.transpose(jnp.broadcast_to(scale, (LANES, batch)))
 
-    ket(1)
     multiply(0)
+    relay()
     x_step(0, 0)
+    ket(2)
     multiply(1)
     x_step(1, 0)
-    ket(2)
+    ket(3)
     x_step(0, 1)
     multiply(2)
     x_step(2, 0)
     x_step(1, 1)
-    ket(3)
+    ket(4)
     x_step(0, 2)
     multiply(3)
     diag_to_sibling()
     x_step(3, 0)
     x_step(2, 1)
-    ket(4)
+    ket(5)
     x_step(1, 2)
     x_step(0, 3)
     diag_to_band()
     x_step(3, 1)
     x_step(2, 2)
-    ket(5)
+    ket(6)
     x_step(1, 3)
     diag_last()
     finish(0)
     x_step(3, 2)
     x_step(2, 3)
-    ket(6)
+    ket(7)
     finish(1)
     x_step(3, 3)
-    ket(7)
+    ket(8)
     finish(2)
     ket_last()
     finish(3)
@@ -512,9 +541,10 @@
             pltpu.VMEM((PIVOT_GROUPS, nx, grows, rows_here), f32),
             pltpu.VMEM((x_messages, grows, rows_here), f32),
             pltpu.VMEM((x_messages, grows, rows_here), f32),
+            pltpu.VMEM((2, 1, block_rows, batch), bf16),
             pltpu.VMEM((2, blocks, block_rows, batch), bf16),
-            pltpu.VMEM((zr, blocks, block_rows, batch), bf16),
-            pltpu.VMEM((zl, blocks, block_rows, batch), bf16),
+            pltpu.VMEM((1 + (zr - 1) * blocks, block_rows, batch), bf16),
+            pltpu.VMEM((1 + (zl - 1) * blocks, block_rows, batch), bf16),
             pltpu.VMEM((1, batch), f32),
             pltpu.VMEM((1, batch), f32),
             pltpu.VMEM((1, batch), f32),
@@ -527,7 +557,7 @@
             dma((1,)),
             dma((1,)),
             dma((1,)),
-            dma((PIVOT_GROUPS,)),
+            dma((PIVOT_GROUPS + 2,)),
             dma((1,)),
             dma((PIVOT_GROUPS, half)),
             dma((1,)),
@@ -535,9 +565,9 @@
             dma((1,)),
             dma((x_messages,)),
             dma((1,)),
-            dma((zr, blocks)),
-            dma((1,)),
-            dma((zl, blocks)),
+            dma((1 + (zr - 1) * blocks,)),
+            dma((1,)),
+            dma((1 + (zl - 1) * blocks,)),
             dma((1,)),
             dma((1,)),
             dma((1,)),

time: 96.3 us -> 95.6 us (level)
  no operation moved by 1% of the time
where the time goes in v4:
time: 95.6 us; the launch traced here: 95.4 us
  Pallas kernels  94.8 us (99%)
    pallas_call x1, Pallas kernels, body(): pl.pallas_call(functools.partial(kernel, nz, nx), out_shape=(pltpu.VMEM((...  94.1 us

profile of v4, /device:TPU:80, one launch (start us, length us, event | category | flops | bytes accessed | tf_op | source)
XLA Modules:
  0.0 95.4 jit_solution(18411428217451710319)
XLA Ops:
  0.6 94.1 %downdate.1 = (bf16[256,256]{1,0:T(8,128)(2,1)S(1)}, f32[1,256]{1,0:T(1,128)S(1)}, bf16[256,256]{1,0:T(8,128)(2,1)S(1)}) custom-call(bf16[192,4096]{1,0:T(8,128)(2,1)} %v_hbm.1, bf16[256,256]{1,0:T(8,128)(2,1)} %prev_hbm.1, s32[1,256]{1,0:T(1,128)} %bitcast.5, f32[1,256]{1,0:T(1,128)} %bitcast.6, bf16[4,128,256]{2,1,0:T(8,128)(2,1)} %ket_hbm.1, ...), custom_call_target="tpu_custom_call" | custom-call | tf_op jit(solution)/shard_map/downdate/pallas_call | solution.py:515
  94.7 0.7 write_out.1
